TPU v7x, 32 devices: a whole 2x2x4 slice. The times are simulated.
32 devices in a mesh: expert: 4 (over y, core), shard: 8 (over z, x).
Axes of the slice: x: 2, y: 2, z: 4, core: 2. Of those that a mesh axis runs over, the one named last changes fastest.
Arguments:
- activations: bfloat16 [4, 8, 96, 2048], P('expert', 'shard'), may hold values from -6 to 6
- out_grads: bfloat16 [4, 8, 96, 7168], P('expert', 'shard'), may hold values from -6 to 6
- next_inputs: bfloat16 [4, 8, 96, 2048], P('expert', 'shard'), may hold values from -6 to 6
- counts: int32 [4, 8], P('expert', 'shard'), may hold values from 1 to 96, as said below
- master: float32 [4, 8, 2048, 896], P('expert', 'shard'), may hold values from -0.125 to 0.125
- moment: bfloat16 [4, 8, 2048, 896], P('expert', 'shard'), may hold values from -6 to 6
- second: bfloat16 [4, 8, 2048, 896], P('expert', 'shard'), may hold values from 0.099609375 to 4
Outputs:
- master_new: float32 [4, 8, 2048, 896], P('expert', 'shard')
- moment_new: bfloat16 [4, 8, 2048, 896], P('expert', 'shard')
- second_new: bfloat16 [4, 8, 2048, 896], P('expert', 'shard')
- projected: bfloat16 [4, 8, 96, 7168], P('expert', 'shard')
Inputs may be any that keep to these rules, and one draw needn't show every extreme that they name: counts[e, s] of the 96 slots of expert e from shard s hold tokens, the leading ones; the rest are padding.
All inputs are finite; a program needn't handle non-finite values.
Results may differ from a plain program's by a relative error of at most 0.00055.
The roundings to bfloat16 on the way count: a program that leaves them out, or rounds other values in their place, can miss the bound.
Values may be sent and summed in bfloat16 or wider, within the bound.
A program may use at most 192 MiB of HBM per device.

v0:
```python
import functools
import jax
import jax.numpy as jnp
from jax import lax
from jax.experimental import pallas as pl
from jax.experimental.pallas import tpu as pltpu
from jax.sharding import PartitionSpec as P

MESH = pl.DeviceIdType.MESH
LANES = 128
SUBLANES = 8


def columns_of(n):
    nx = 1
    while n % (2 * nx) == 0 and 8 * nx * nx <= n:
        nx *= 2
    return nx


def fold(x):
    rows, cols = x.shape
    x = jnp.sum(x.reshape(rows // SUBLANES, SUBLANES, cols), axis=0)
    acc = x[:, 0:LANES]
    for c in range(LANES, cols, LANES):
        acc = acc + x[:, c : c + LANES]
    return acc


def greet(axes):
    barrier = pltpu.get_barrier_semaphore()
    total = 0
    for name, size in axes:
        mine = lax.axis_index(name)
        for d in range(1, size):
            peer = lax.rem(mine + d, size)
            pl.semaphore_signal(barrier, inc=1, device_id={name: peer}, device_id_type=MESH)
        total += size - 1
    pl.semaphore_wait(barrier, total)


def step_kernel(
    n, ne, nx, grid_c, entries,
    act, cots, nxt, w_hbm, m_hbm, v_hbm,
    w_out, m_out, v_out, wb_out, nxt_all,
    acts, cot_all, w, m, v, sq_src, sq_all, ex_src, ex_all, up_src, up_all,
    load_sem, own_sem,
    az_send, az_recv, ax_send, ax_recv, nz_send, nz_recv, nx_send, nx_recv,
    cot_send, cot_recv, sq_send, sq_recv, ex_send, ex_recv, up_send, up_recv,
):
    nz = n // nx
    me = lax.axis_index("shard")
    ex = lax.axis_index("expert")
    iz, ix = me // nx, lax.rem(me, nx)
    cap, d_full = act.shape
    d_blk, f_blk = w.shape
    half = cap // 2
    row0 = pl.multiple_of((me // grid_c) * d_blk, d_blk)

    loads = [
        pltpu.make_async_copy(src, dst, load_sem.at[i])
        for i, (src, dst) in enumerate(((w_hbm, w), (m_hbm, m), (v_hbm, v)))
    ]
    owns = [
        pltpu.make_async_copy(act, acts.at[me], own_sem.at[0]),
        pltpu.make_async_copy(nxt, nxt_all.at[me], own_sem.at[1]),
        pltpu.make_async_copy(cots.at[lax.rem(me, grid_c)], cot_all.at[me], own_sem.at[2]),
    ]
    for c in owns + loads:
        c.start()
    greet((("shard", n), ("expert", ne)))
    owns[0].wait()
    owns[1].wait()

    sends = []

    def send(src, dst, s, r, peer, axis="shard", when=None):
        c = pltpu.make_async_remote_copy(
            src_ref=src, dst_ref=dst, send_sem=s, recv_sem=r,
            device_id={axis: peer}, device_id_type=MESH,
        )
        if when is None:
            c.start()
        else:
            pl.when(when)(c.start)
        sends.append((when, c))

    def z_slot(k):
        return lax.rem(iz + k + nz, nz) * nx + ix

    def part(buf, slot, p):
        return buf.at[slot, pl.ds(p * half, half)]

    def holds(h, t):
        return iz >= t if h == 0 else iz < nz - t

    def z_send(buf, t, h, p, zs, zr):
        way = 1 - 2 * h
        slot = z_slot(-way * (t - 1))
        more = jnp.logical_and(iz >= t - 1, iz < nz - 1) if h == 0 else jnp.logical_and(iz <= nz - t, iz > 0)
        send(part(buf, slot, p), part(buf, slot, p), zs.at[h, p, t], zr.at[h, p, t], z_slot(way), when=more)

    def x_send(buf, t, h, p, xs, xr):
        way = 1 - 2 * h
        slot = z_slot(-way * t)
        for d in range(1, nx):
            peer = iz * nx + lax.rem(ix + d, nx)
            send(
                part(buf, slot, p), part(buf, slot, p), xs.at[h, p, t, d], xr.at[h, p, t, d], peer,
                when=None if t == 0 else holds(h, t),
            )

    def arrived(buf, slot, p, sem, when=None):
        ref = part(buf, slot, p)
        c = pltpu.make_async_copy(ref, ref, sem)
        if when is None:
            c.wait()
        else:
            pl.when(when)(c.wait)

    def own_sends(buf, zs, zr, xs, xr):
        for p in range(2):
            if nz > 1:
                for h in range(2):
                    z_send(buf, 1, h, p, zs, zr)
            x_send(buf, 0, 0, p, xs, xr)

    def relay(buf, t, zs, zr, xs, xr):
        for p in range(2):
            for h in range(2):
                arrived(buf, z_slot(-(1 - 2 * h) * t), p, zr.at[h, p, t], when=holds(h, t))
                if t < nz - 1:
                    z_send(buf, t + 1, h, p, zs, zr)
                x_send(buf, t, h, p, xs, xr)

    def finish(buf, xr):
        for t in range(nz):
            for h in range(2 if t else 1):
                for p in range(2):
                    for d in range(1, nx):
                        slot = lax.rem(iz - (1 - 2 * h) * t + nz, nz) * nx + lax.rem(ix - d + nx, nx)
                        arrived(buf, slot, p, xr.at[h, p, t, d], when=holds(h, t) if t else None)

    def cot_sends(ds):
        for d in ds:
            peer = lax.rem(me + d, n)
            send(cots.at[lax.rem(peer, grid_c)], cot_all.at[me], cot_send.at[d], cot_recv.at[d], peer)

    acts_sems = (az_send, az_recv, ax_send, ax_recv)
    nxt_sems = (nz_send, nz_recv, nx_send, nx_recv)
    own_sends(acts, *acts_sems)
    order = sorted(range(1, n), key=lambda d: -min(d, n - d))
    share = -(-len(order) // nz)
    cot_sends(order[:share])
    for t in range(1, nz):
        relay(acts, t, *acts_sems)
        cot_sends(order[share * t : share * (t + 1)])
    own_sends(nxt_all, *nxt_sems)

    tile = 64
    loads[0].wait()

    def w_body(i, acc):
        x = w[pl.ds(i * tile, tile), :]
        return acc + fold(x * x)

    zero = jnp.zeros((SUBLANES, LANES), jnp.float32)
    up_src[0] = lax.fori_loop(0, d_blk // tile, w_body, zero)
    loads[1].wait()
    loads[2].wait()
    finish(acts, ax_recv)
    owns[2].wait()
    for d in range(1, n):
        slot = lax.rem(me - d + n, n)
        pltpu.make_async_copy(cot_all.at[slot], cot_all.at[slot], cot_recv.at[d]).wait()

    g_tile = 256

    def g_body(i, acc):
        a = acts[:, :, pl.ds(pl.multiple_of(row0 + i * g_tile, g_tile), g_tile)]
        g = lax.dot_general(
            a.reshape(n * cap, g_tile), cot_all[...].reshape(n * cap, f_blk),
            (((0,), (0,)), ((), ())), preferred_element_type=jnp.float32,
        )
        w_out[pl.ds(pl.multiple_of(i * g_tile, g_tile), g_tile), :] = g
        return acc + fold(g * g)

    sq_src[...] = lax.fori_loop(0, d_blk // g_tile, g_body, zero)

    def spread(src, dst, ss, rs, axis, mine, size):
        for d in range(1, size):
            send(src, dst.at[mine], ss.at[d], rs.at[d], lax.rem(mine + d, size), axis)

    def collect(src, dst, rs, mine, size):
        total = src[...]
        for d in range(1, size):
            slot = lax.rem(mine - d + size, size)
            pltpu.make_async_copy(dst.at[slot], dst.at[slot], rs.at[d]).wait()
            total = total + dst[slot]
        return total

    spread(sq_src, sq_all, sq_send, sq_recv, "shard", me, n)
    if nz > 1:
        relay(nxt_all, 1, *nxt_sems)
    ex_src[...] = collect(sq_src, sq_all, sq_recv, me, n)
    spread(ex_src, ex_all, ex_send, ex_recv, "expert", ex, ne)
    norm_total = jnp.sum(collect(ex_src, ex_all, ex_recv, ex, ne), keepdims=True)
    rms = jnp.sqrt(norm_total / entries + 1e-06)
    clip = jnp.minimum(1.0, 1.0 / rms)
    for t in range(2, nz):
        if t < nz - 1:
            relay(nxt_all, t, *nxt_sems)

    u_tile = 32

    def u_body(i, acc):
        rows = pl.ds(pl.multiple_of(i * u_tile, u_tile), u_tile)
        g = clip * w_out[rows, :]
        m_new = 0.9 * m[rows, :].astype(jnp.float32) + 0.1 * g
        v_new = 0.999 * v[rows, :].astype(jnp.float32) + 0.001 * g * g
        m_out[rows, :] = m_new.astype(jnp.bfloat16)
        v_out[rows, :] = v_new.astype(jnp.bfloat16)
        scaled = m_new * (1.0 / (1.0 - 0.9**10))
        root = jnp.sqrt(v_new * (1.0 / (1.0 - 0.999**10)))
        u = scaled / (root + 1e-06) + 0.01 * w[rows, :]
        w_out[rows, :] = u
        return acc + fold(u * u)

    up_src[1] = lax.fori_loop(0, d_blk // u_tile, u_body, zero)
    spread(up_src, up_all, up_send, up_recv, "shard", me, n)
    if nz > 2:
        relay(nxt_all, nz - 1, *nxt_sems)
    sums = collect(up_src, up_all, up_recv, me, n)
    trust = jnp.sqrt(jnp.sum(sums[0], keepdims=True)) / (
        jnp.sqrt(jnp.sum(sums[1], keepdims=True)) + 1e-06
    )
    rate = 0.08 * trust

    def p_body(i, carry):
        rows = pl.ds(pl.multiple_of(i * u_tile, u_tile), u_tile)
        x = w[rows, :] - rate * w_out[rows, :]
        w_out[rows, :] = x
        wb_out[rows, :] = x.astype(jnp.bfloat16)
        return carry

    lax.fori_loop(0, d_blk // u_tile, p_body, 0)
    finish(nxt_all, nx_recv)
    for when, c in sends:
        if when is None:
            c.wait_send()
        else:
            pl.when(when)(c.wait_send)


def project_kernel(n, grid_c, chunks, nxt_all, wb, got, made, own_sem, send_sem, recv_sem):
    me = lax.axis_index("shard")
    d_blk, f_blk = wb.shape
    cap = nxt_all.shape[1]
    row0 = pl.multiple_of((me // grid_c) * d_blk, d_blk)
    greet((("shard", n),))
    copies = []
    start = 0
    for k, width in enumerate(chunks):
        cols = pl.ds(start, width)
        x = nxt_all[:, :, pl.ds(row0, d_blk)].reshape(n * cap, d_blk)
        y = jnp.dot(x, wb[:, cols], preferred_element_type=jnp.float32)
        made[:, :, cols] = y.astype(made.dtype).reshape(n, cap, width)
        for d in range(1, n):
            peer = lax.rem(me + d, n)
            c = pltpu.make_async_remote_copy(
                src_ref=made.at[peer, :, cols], dst_ref=got.at[me, :, cols],
                send_sem=send_sem.at[k, d], recv_sem=recv_sem.at[k, d],
                device_id={"shard": peer}, device_id_type=MESH,
            )
            c.start()
            copies.append(c)
        start += width
    own = pltpu.make_async_copy(made.at[me], got.at[me], own_sem.at[0])
    own.start()
    own.wait()
    start = 0
    for k, width in enumerate(chunks):
        for d in range(1, n):
            ref = got.at[lax.rem(me - d + n, n), :, pl.ds(start, width)]
            pltpu.make_async_copy(ref, ref, recv_sem.at[k, d]).wait()
        start += width
    for c in copies:
        c.wait_send()


def store_kernel(*refs):
    count = len(refs) // 2
    sems = refs[-1]
    copies = [pltpu.make_async_copy(refs[i], refs[count + i], sems.at[i]) for i in range(count)]
    for c in copies:
        c.start()
    for c in copies:
        c.wait()


def split_lanes(f_blk, parts):
    units = f_blk // LANES
    parts = min(parts, units)
    return tuple((units // parts + (1 if i >= parts - units % parts else 0)) * LANES for i in range(parts))


def body(activations, out_grads, next_inputs, counts, master, moment, second):
    n = lax.axis_size("shard")
    ne = lax.axis_size("expert")
    cap, d_full = activations.shape[2:]
    ff = out_grads.shape[3]
    d_blk, f_blk = master.shape[2:]
    grid_r, grid_c = d_full // d_blk, ff // f_blk
    nx = columns_of(n)
    nz = n // nx
    entries = float(ne * master.shape[0] * d_full * ff)
    valid = lax.iota(jnp.int32, cap) < counts[0, 0]
    masked = jnp.where(valid[:, None], out_grads[0, 0], jnp.zeros((), jnp.bfloat16))
    cots = masked.reshape(cap, grid_c, f_blk).transpose(1, 0, 2)

    f32, bf16 = jnp.float32, jnp.bfloat16
    any_spec = pl.BlockSpec(memory_space=pl.ANY)
    vmem_spec = pl.BlockSpec(memory_space=pltpu.VMEM)
    dma = pltpu.SemaphoreType.DMA
    sq = (SUBLANES, LANES)
    w_new, m_new, v_new, wb, nxt_all = pl.pallas_call(
        functools.partial(step_kernel, n, ne, nx, grid_c, entries),
        out_shape=(
            pltpu.VMEM((d_blk, f_blk), f32),
            pltpu.VMEM((d_blk, f_blk), bf16),
            pltpu.VMEM((d_blk, f_blk), bf16),
            pltpu.VMEM((d_blk, f_blk), bf16),
            pltpu.VMEM((n, cap, d_full), bf16),
        ),
        in_specs=[any_spec] * 3 + [pl.BlockSpec(memory_space=pltpu.HBM)] * 3,
        out_specs=(vmem_spec,) * 5,
        scratch_shapes=[
            pltpu.VMEM((n, cap, d_full), bf16),
            pltpu.VMEM((n, cap, f_blk), bf16),
            pltpu.VMEM((d_blk, f_blk), f32),
            pltpu.VMEM((d_blk, f_blk), bf16),
            pltpu.VMEM((d_blk, f_blk), bf16),
            pltpu.VMEM(sq, f32),
            pltpu.VMEM((n,) + sq, f32),
            pltpu.VMEM(sq, f32),
            pltpu.VMEM((ne,) + sq, f32),
            pltpu.VMEM((2,) + sq, f32),
            pltpu.VMEM((n, 2) + sq, f32),
            dma((3,)),
            dma((3,)),
        ]
        + [dma((2, 2, nz)), dma((2, 2, nz)), dma((2, 2, nz, nx)), dma((2, 2, nz, nx))] * 2
        + [dma((n,)), dma((n,)), dma((n,)), dma((n,)), dma((ne,)), dma((ne,)), dma((n,)), dma((n,))],
        compiler_params=pltpu.CompilerParams(
            collective_id=0, has_side_effects=True, vmem_limit_bytes=26 * 2**20
        ),
    )(activations[0, 0], cots, next_inputs[0, 0], master[0, 0], moment[0, 0], second[0, 0])

    w_new, m_new, v_new = pl.pallas_call(
        store_kernel,
        out_shape=tuple(jax.ShapeDtypeStruct(x.shape, x.dtype) for x in (w_new, m_new, v_new)),
        in_specs=[vmem_spec] * 3,
        out_specs=(any_spec,) * 3,
        scratch_shapes=[dma((3,))],
        compiler_params=pltpu.CompilerParams(vmem_limit_bytes=2**20),
    )(w_new, m_new, v_new)

    back = bf16 if grid_r == 1 else f32
    chunks = split_lanes(f_blk, 3)
    got = pl.pallas_call(
        functools.partial(project_kernel, n, grid_c, chunks),
        out_shape=jax.ShapeDtypeStruct((n, cap, f_blk), back),
        in_specs=[vmem_spec] * 2,
        out_specs=vmem_spec,
        scratch_shapes=[
            pltpu.VMEM((n, cap, f_blk), back),
            dma((1,)),
            dma((len(chunks), n)),
            dma((len(chunks), n)),
        ],
        compiler_params=pltpu.CompilerParams(
            collective_id=1, has_side_effects=True, vmem_limit_bytes=16 * 2**20
        ),
    )(nxt_all, wb)
    summed = jnp.sum(got.reshape(grid_r, grid_c, cap, f_blk), axis=0)
    projected = summed.transpose(1, 0, 2).reshape(cap, ff).astype(bf16)
    return w_new[None, None], m_new[None, None], v_new[None, None], projected[None, None]


def solution(mesh):
    spec = P("expert", "shard", None, None)
    return jax.shard_map(
        body,
        mesh=mesh,
        in_specs=(spec, spec, spec, P("expert", "shard"), spec, spec, spec),
        out_specs=(spec,) * 4,
        check_vma=False,
    )
```

profile of v0, /device:TPU:0, one launch (start us, length us, event | category | flops | bytes accessed | tf_op | source)
XLA Modules:
  0.0 143.7 jit_solution(16066047688603764064)
XLA Ops:
  0.6 0.0 copy-start
  0.6 0.0 copy-start.2
  0.7 0.0 copy-start.1
  1.5 2.0 %copy.13 = bf16[12,8,8,896]{3,2,1,0:T(8,128)(2,1)S(1)} copy(bf16[12,8,8,896]{3,1,2,0:T(8,128)(2,1)} %bitcast.24) | data formatting | bytes 2752512
  3.5 0.3 fusion.cots
  3.8 0.0 copy-done
  3.8 0.0 copy-done.2
  3.8 0.0 copy-done.1
  3.8 100.2 %shard_map.102 = (f32[2048,896]{1,0:T(8,128)S(1)}, bf16[2048,896]{1,0:T(8,128)(2,1)S(1)}, bf16[2048,896]{1,0:T(8,128)(2,1)S(1)}, bf16[2048,896]{1,0:T(8,128)(2,1)S(1)}, bf16[8,96,2048]{2,1,0:T(8,128)(2,1)S(1)}) custom-call(bf16[96,2048]{1,0:T(8,128)(2,1)S(1)} %bitcast.19, bf16[8,96,896]{2,1,0:T(8,128)(2,1)S(1)} %fusion.cots, bf16[96,2048]{1,0:T(8,128)(2,1)S(1)} %bitcast.20, ...), custom_call_target="tpu_custom_call" | custom-call | tf_op jit(solution)/shard_map/pallas_call | solution.py:326
  104.0 5.4 %shard_map.103 = (f32[2048,896]{1,0:T(8,128)}, bf16[2048,896]{1,0:T(8,128)(2,1)}, bf16[2048,896]{1,0:T(8,128)(2,1)}) custom-call(f32[2048,896]{1,0:T(8,128)S(1)} %get-tuple-element.12.refs_0_, bf16[2048,896]{1,0:T(8,128)(2,1)S(1)} %get-tuple-element.13.refs_1_, bf16[2048,896]{1,0:T(8,128)(2,1)S(1)} %get-tuple-element.14.refs_2_), custom_call_target="tpu_custom_call" | custom-call | tf_op jit(solution)/shard_map/pallas_call | solution.py:359
  109.4 32.4 %shard_map.104 = bf16[8,96,896]{2,1,0:T(8,128)(2,1)S(1)} custom-call(bf16[8,96,2048]{2,1,0:T(8,128)(2,1)S(1)} %get-tuple-element.18.nxt_all, bf16[2048,896]{1,0:T(8,128)(2,1)S(1)} %get-tuple-element.19.wb), custom_call_target="tpu_custom_call" | custom-call | tf_op jit(solution)/shard_map/pallas_call | solution.py:370
  141.8 0.4 copy.12
  142.2 1.5 %broadcast_in_dim_reshape.3 = bf16[1,1,96,7168]{3,2,1,0:T(8,128)(2,1)} reshape(bf16[96,8,896]{2,1,0:T(8,128)(2,1)S(1)} %copy.12) | data formatting | bytes 2752512 | tf_op jit(solution)/shard_map/broadcast_in_dim;reshape | solution.py:387
  (1 shorter events, 0.0 us)
Async XLA Ops:
  0.6 3.2 %copy-start = (bf16[1,1,2048,896]{3,2,1,0:T(8,128)(2,1)S(1)}, bf16[1,1,2048,896]{3,2,1,0:T(8,128)(2,1)}, u32[]{:S(2)}) copy-start(bf16[1,1,2048,896]{3,2,1,0:T(8,128)(2,1)} %param.12) | copy-start | bytes 11010052
  0.6 3.2 %copy-start.2 = (bf16[1,1,96,2048]{3,2,1,0:T(8,128)(2,1)S(1)}, bf16[1,1,96,2048]{3,2,1,0:T(8,128)(2,1)}, u32[]{:S(2)}) copy-start(bf16[1,1,96,2048]{3,2,1,0:T(8,128)(2,1)} %param.9) | copy-start | bytes 1179652
  0.7 3.2 %copy-start.1 = (bf16[1,1,96,2048]{3,2,1,0:T(8,128)(2,1)S(1)}, bf16[1,1,96,2048]{3,2,1,0:T(8,128)(2,1)}, u32[]{:S(2)}) copy-start(bf16[1,1,96,2048]{3,2,1,0:T(8,128)(2,1)} %param.7) | copy-start | bytes 1179652
where the time goes:
time: 144 us
  Pallas kernels  138 us (96%)
  local copies, waits for them, and re-layouts  3.94 us (3%)
  between operations  1.53 us (1%)
    pallas_call x1, Pallas kernels, body(): pl.pallas_call(functools.partial(step_kernel, n, ne, nx, grid_c, entries)...  100 us
    pallas_call x1, Pallas kernels, body(): pl.pallas_call(functools.partial(project_kernel, n, grid_c, chunks), out_...  32.4 us
    pallas_call x1, Pallas kernels, body(): pl.pallas_call(store_kernel, out_shape=tuple((jax.ShapeDtypeStruct(x.shap...  5.38 us

commit v1 on v0

--- a/solution.py
+++ b/solution.py
@@ -304,7 +304,7 @@
     return tuple((units // parts + (1 if i >= parts - units % parts else 0)) * LANES for i in range(parts))
 
 
-def body(activations, out_grads, next_inputs, counts, master, moment, second):
+def split_body(activations, out_grads, next_inputs, counts, master, moment, second):
     n = lax.axis_size("shard")
     ne = lax.axis_size("expert")
     cap, d_full = activations.shape[2:]
@@ -387,6 +387,380 @@
     return w_new[None, None], m_new[None, None], v_new[None, None], projected[None, None]
 
 
+def flip(z, k, top):
+    out, bit = z, 1
+    while bit < top:
+        out = out + lax.rem(lax.div(k, bit), 2) * bit * (1 - 2 * lax.rem(lax.div(z, bit), 2))
+        bit *= 2
+    return out
+
+
+def fused_kernel(
+    n, ne, nx, entries, parts, halves, pieces,
+    cnt_hbm, act, cot_hbm, nxt, w_hbm, m_hbm, v_hbm,
+    w_out, m_out, v_out, got,
+    acts, nxt_all, cot_all, cots, w, wb, cnt, sq_src, sq_all, up_src, up_all,
+    load_sem,
+    az_send, az_recv, ax_send, ax_recv, nz_send, nz_recv, nx_send, nx_recv,
+    cot_sem, sq_sem, up_sem, y_sem,
+):
+    nz = n // nx
+    me = lax.axis_index("shard")
+    ex = lax.axis_index("expert")
+    iz, ix = lax.div(me, nx), lax.rem(me, nx)
+    cap, d_full = act.shape
+    d_blk, f_blk = w.shape
+
+    barrier = pltpu.get_barrier_semaphore()
+    for de in range(ne):
+        for ds in range(n):
+            if de or ds:
+                pl.semaphore_signal(
+                    barrier, inc=1, device_id_type=MESH,
+                    device_id={"expert": lax.rem(ex + de, ne), "shard": lax.rem(me + ds, n)},
+                )
+    loads = [
+        pltpu.make_async_copy(src, dst, load_sem.at[i])
+        for i, (src, dst) in enumerate((
+            (cnt_hbm, cnt), (act, acts.at[me]), (cot_hbm, cots), (nxt, nxt_all.at[me]),
+            (w_hbm, w), (m_hbm, m_out), (v_hbm, v_out),
+        ))
+    ]
+    for c in loads:
+        c.start()
+    loads[0].wait()
+    loads[1].wait()
+    loads[2].wait()
+    valid = lax.broadcasted_iota(jnp.int32, (cap, f_blk), 0) < cnt[...]
+
+    def mask_body(j, carry):
+        cols = pl.ds(pl.multiple_of(j * f_blk, LANES), f_blk)
+        x = cots[:, cols].astype(jnp.float32)
+        cots[:, cols] = jnp.where(valid, x, 0.0).astype(jnp.bfloat16)
+        return carry
+
+    lax.fori_loop(0, n, mask_body, 0)
+    pl.semaphore_wait(barrier, ne * n - 1)
+
+    drains = []
+
+    def send(src, dst, s, r, shard, expert=None, when=None):
+        device = {"shard": shard} if expert is None else {"expert": expert, "shard": shard}
+        c = pltpu.make_async_remote_copy(
+            src_ref=src, dst_ref=dst, send_sem=s, recv_sem=r, device_id=device, device_id_type=MESH,
+        )
+        if when is None:
+            c.start()
+        else:
+            pl.when(when)(c.start)
+
+    def await_copy(ref, sem, when=None):
+        c = pltpu.make_async_copy(ref, ref, sem)
+        if when is None:
+            c.wait()
+        else:
+            pl.when(when)(c.wait)
+
+    def z_slot(k):
+        return lax.rem(iz + k + nz, nz) * nx + ix
+
+    def cut(buf, slot, p, count):
+        width = d_full // count
+        return buf.at[slot, :, pl.ds(p * width, width)]
+
+    def holds(h, t):
+        return iz >= t if h == 0 else iz < nz - t
+
+    def z_send(g, t, h, p):
+        buf, count, zs, zr, _, _ = g
+        way = 1 - 2 * h
+        slot = z_slot(-way * (t - 1))
+        more = jnp.logical_and(iz >= t - 1, iz < nz - 1) if h == 0 else jnp.logical_and(iz <= nz - t, iz > 0)
+        block = cut(buf, slot, p, count)
+        send(block, block, zs.at[h, t], zr.at[h, p, t], z_slot(way), when=more)
+        if p == 0:
+            drains.append((buf.at[slot], zs.at[h, t], more))
+
+    def x_send(g, t, h, p):
+        buf, count, _, _, xs, xr = g
+        slot = z_slot(-(1 - 2 * h) * t)
+        when = None if t == 0 else holds(h, t)
+        block = cut(buf, slot, p, count)
+        for d in range(1, nx):
+            landing = xr.at[p] if buf is acts else xr.at[h, t, d - 1]
+            send(block, block, xs.at[h, t, d - 1], landing, iz * nx + lax.rem(ix + d, nx), when=when)
+            if p == 0:
+                drains.append((buf.at[slot], xs.at[h, t, d - 1], when))
+
+    def own_z(g, p):
+        if nz > 1:
+            for h in range(2):
+                z_send(g, 1, h, p)
+
+    def own(g, ps):
+        for p in ps:
+            own_z(g, p)
+            x_send(g, 0, 0, p)
+
+    def relay(g, t, ps):
+        for p in ps:
+            for h in range(2):
+                await_copy(cut(g[0], z_slot(-(1 - 2 * h) * t), p, g[1]), g[3].at[h, p, t], holds(h, t))
+                if t < nz - 1:
+                    z_send(g, t + 1, h, p)
+                x_send(g, t, h, p)
+
+    def peer_to(k, dx):
+        return flip(iz, k, nz) * nx + lax.rem(ix + dx, nx)
+
+    def cot_sends(which):
+        for k, dx in which:
+            peer = peer_to(k, dx)
+            cols = pl.ds(pl.multiple_of(peer * f_blk, LANES), f_blk)
+            send(cots.at[:, cols], cot_all.at[me], cot_sem.at[0], cot_sem.at[1], peer)
+
+    g_acts = (acts, parts, az_send, az_recv, ax_send, ax_recv)
+    g_nxt = (nxt_all, halves, nz_send, nz_recv, nx_send, nx_recv)
+    every, each = range(parts), range(halves)
+    tile = 64
+
+    def w_body(i, acc):
+        x = w[pl.ds(pl.multiple_of(i * tile, tile), tile), :]
+        return acc + fold(x * x)
+
+    zero = jnp.zeros((SUBLANES, LANES), jnp.float32)
+    far = sorted(range(1, nz), key=lambda k: (-k.bit_length(), k))
+    near = [(0, dx) for dx in range(1, nx)]
+    order = near + [(k, 0) for k in far] + [(k, dx) for k in far for dx in range(1, nx)]
+    share = -(-len(order) // max(nz - 1, 1))
+    cuts = [share * (t + 1) for t in range(nz)]
+
+    own(g_acts, every)
+    cot_sends(order[: cuts[0]])
+    cot_all[me] = cots[:, pl.ds(pl.multiple_of(me * f_blk, LANES), f_blk)]
+    squares = zero
+    for t in range(1, nz):
+        relay(g_acts, t, every)
+        cot_sends(order[cuts[t - 1] : cuts[t]])
+        if t == 1:
+            loads[4].wait()
+            squares = lax.fori_loop(0, d_blk // tile, w_body, zero)
+    up_src[0:1] = jnp.sum(squares, axis=0, keepdims=True)
+    await_copy(cot_all.at[pl.ds(0, n - 1)], cot_sem.at[1])
+
+    g_tile = 256
+    total = zero
+    per = d_full // parts // g_tile
+
+    def g_body(i, acc):
+        rows = pl.ds(pl.multiple_of(i * g_tile, g_tile), g_tile)
+        g = lax.dot_general(
+            acts[:, :, rows].reshape(n * cap, g_tile), cot_all[...].reshape(n * cap, f_blk),
+            (((0,), (0,)), ((), ())), preferred_element_type=jnp.float32,
+        )
+        w_out[rows, :] = g
+        return acc + fold(g * g)
+
+    for p in every:
+        if nx > 1:
+            width = d_full // parts
+            await_copy(acts.at[pl.ds(0, nz * (nx - 1)), :, pl.ds(p * width, width)], ax_recv.at[p])
+        total = lax.fori_loop(p * per, (p + 1) * per, g_body, total)
+    sq_src[...] = jnp.sum(total, axis=0, keepdims=True)
+    for de in range(ne):
+        for ds in range(n):
+            if de or ds:
+                send(
+                    sq_src, sq_all.at[de * n + ds], sq_sem.at[0], sq_sem.at[1],
+                    lax.rem(me + ds, n), lax.rem(ex + de, ne),
+                )
+    loads[3].wait()
+    own(g_nxt, each)
+    loads[5].wait()
+    loads[6].wait()
+    await_copy(sq_all.at[pl.ds(1, ne * n - 1)], sq_sem.at[1])
+    norm = sq_src[...]
+    for k in range(1, ne * n):
+        norm = norm + sq_all[k]
+    rms = jnp.sqrt(jnp.sum(norm, keepdims=True) / entries + 1e-06)
+    clip = jnp.minimum(1.0, 1.0 / rms)
+
+    u_tile = 32
+    first_scale, later_scale = 1.0 / (1.0 - 0.9**10), 1.0 / (1.0 - 0.999**10)
+
+    def u_body(i, acc):
+        rows = pl.ds(pl.multiple_of(i * u_tile, u_tile), u_tile)
+        g = clip * w_out[rows, :]
+        m_new = 0.9 * m_out[rows, :].astype(jnp.float32) + 0.1 * g
+        v_new = 0.999 * v_out[rows, :].astype(jnp.float32) + 0.001 * g * g
+        m_out[rows, :] = m_new.astype(jnp.bfloat16)
+        v_out[rows, :] = v_new.astype(jnp.bfloat16)
+        later = v_new * later_scale
+        root = later * lax.rsqrt(later)
+        u = (m_new * first_scale) / (root + 1e-06) + 0.01 * w[rows, :]
+        w_out[rows, :] = u
+        return acc + fold(u * u)
+
+    def u_span(first, last, acc):
+        return lax.fori_loop(first, last, u_body, acc)
+
+    steps = d_blk // u_tile
+    early = 1
+    mid = steps * 3 // 4
+    acc = u_span(0, mid, zero)
+    if nz > 1:
+        relay(g_nxt, 1, each[:early])
+    acc = u_span(mid, steps, acc)
+    up_src[1:2] = jnp.sum(acc, axis=0, keepdims=True)
+    for ds in range(1, n):
+        send(up_src, up_all.at[ds], up_sem.at[0], up_sem.at[1], lax.rem(me + ds, n))
+    if nz > 1:
+        relay(g_nxt, 1, each[early:])
+    await_copy(up_all.at[pl.ds(1, n - 1)], up_sem.at[1])
+    sums = up_src[...]
+    for ds in range(1, n):
+        sums = sums + up_all[ds]
+    trust = jnp.sqrt(jnp.sum(sums[0:1], keepdims=True)) / (jnp.sqrt(jnp.sum(sums[1:2], keepdims=True)) + 1e-06)
+    rate = 0.08 * trust
+
+    def p_body(i, carry):
+        rows = pl.ds(pl.multiple_of(i * u_tile, u_tile), u_tile)
+        x = w[rows, :] - rate * w_out[rows, :]
+        w_out[rows, :] = x
+        wb[rows, :] = x.astype(jnp.bfloat16)
+        return carry
+
+    lax.fori_loop(0, steps, p_body, 0)
+
+    def crossed(t):
+        for h in range(2 if t else 1):
+            for d in range(1, nx):
+                slot = lax.rem(iz - (1 - 2 * h) * t + nz, nz) * nx + lax.rem(ix - d + nx, nx)
+                await_copy(nxt_all.at[slot], nx_recv.at[h, t, d - 1], holds(h, t) if t else None)
+
+    def project(k, dx):
+        peer = peer_to(k, dx)
+        start = 0
+        for piece in pieces:
+            cols = pl.ds(start, piece)
+            y = jnp.dot(nxt_all[peer], wb[:, cols], preferred_element_type=jnp.float32)
+            cot_all[peer, :, cols] = y.astype(jnp.bfloat16)
+            if dx or not (isinstance(k, int) and k == 0):
+                mine = pl.ds(pl.multiple_of(me * f_blk + start, LANES), piece)
+                send(cot_all.at[peer, :, cols], got.at[:, mine], y_sem.at[0], y_sem.at[1], peer)
+            start += piece
+
+    if nz == 4:
+        inner = lax.rem(lax.div(iz + 1, 2), 2)
+        ks = [1 + 2 * inner, 2, 3 - 2 * inner]
+    else:
+        ks = far
+    others = range(1, nx)
+    if nz == 4:
+        project(ks[0], 0)
+        relay(g_nxt, 2, each)
+        project(ks[1], 0)
+        crossed(0)
+        crossed(1)
+        for dx in others:
+            project(ks[0], dx)
+        relay(g_nxt, 3, each)
+        project(ks[2], 0)
+        crossed(2)
+        for dx in others:
+            project(ks[1], dx)
+        crossed(3)
+        for dx in others:
+            project(ks[2], dx)
+    else:
+        for t in range(2, nz):
+            relay(g_nxt, t, each)
+        for t in range(nz):
+            crossed(t)
+        for k in ks:
+            for dx in range(nx):
+                project(k, dx)
+    for dx in others:
+        project(0, dx)
+    project(0, 0)
+    got[:, pl.ds(pl.multiple_of(me * f_blk, LANES), f_blk)] = cot_all[me]
+    if n > 1:
+        await_copy(got.at[:, pl.ds(0, (n - 1) * f_blk)], y_sem.at[1])
+        drains.append((got.at[:, pl.ds(0, (n - 1) * f_blk)], y_sem.at[0], None))
+        drains.append((cot_all.at[pl.ds(0, n - 1)], cot_sem.at[0], None))
+        drains.append((up_all.at[pl.ds(1, n - 1)], up_sem.at[0], None))
+    drains.append((sq_all.at[pl.ds(1, ne * n - 1)], sq_sem.at[0], None))
+    for ref, sem, when in drains:
+        await_copy(ref, sem, when)
+
+
+def fused_body(activations, out_grads, next_inputs, counts, master, moment, second):
+    n = lax.axis_size("shard")
+    ne = lax.axis_size("expert")
+    cap, d_full = activations.shape[2:]
+    ff = out_grads.shape[3]
+    d_blk, f_blk = master.shape[2:]
+    nx = columns_of(n)
+    nz = n // nx
+    entries = float(ne * master.shape[0] * d_full * ff)
+    f32, bf16 = jnp.float32, jnp.bfloat16
+    any_spec = pl.BlockSpec(memory_space=pl.ANY)
+    vmem_spec = pl.BlockSpec(memory_space=pltpu.VMEM)
+    dma = pltpu.SemaphoreType.DMA
+    parts = 4
+    pieces = split_lanes(f_blk, 2)
+    halves = 2
+    across = dma((2, nz, max(nx - 1, 1)))
+    results = pl.pallas_call(
+        functools.partial(fused_kernel, n, ne, nx, entries, parts, halves, pieces),
+        out_shape=(
+            pltpu.VMEM((d_blk, f_blk), f32),
+            pltpu.VMEM((d_blk, f_blk), bf16),
+            pltpu.VMEM((d_blk, f_blk), bf16),
+            pltpu.VMEM((cap, ff), bf16),
+        ),
+        in_specs=[pl.BlockSpec(memory_space=pltpu.HBM)] * 7,
+        out_specs=(vmem_spec,) * 4,
+        scratch_shapes=[
+            pltpu.VMEM((n, cap, d_full), bf16),
+            pltpu.VMEM((n, cap, d_full), bf16),
+            pltpu.VMEM((n, cap, f_blk), bf16),
+            pltpu.VMEM((cap, ff), bf16),
+            pltpu.VMEM((d_blk, f_blk), f32),
+            pltpu.VMEM((d_blk, f_blk), bf16),
+            pltpu.VMEM((1, 1), jnp.int32),
+            pltpu.VMEM((1, LANES), f32),
+            pltpu.VMEM((ne * n, 1, LANES), f32),
+            pltpu.VMEM((2, LANES), f32),
+            pltpu.VMEM((n, 2, LANES), f32),
+            dma((7,)),
+        ]
+        + [dma((2, nz)), dma((2, parts, nz)), across, dma((parts,))]
+        + [dma((2, nz)), dma((2, halves, nz)), across, across]
+        + [dma((2,))] * 4,
+        compiler_params=pltpu.CompilerParams(
+            collective_id=0, has_side_effects=True, vmem_limit_bytes=47 * 2**20
+        ),
+    )(counts, activations[0, 0], out_grads[0, 0], next_inputs[0, 0], master[0, 0], moment[0, 0], second[0, 0])
+    outs = pl.pallas_call(
+        store_kernel,
+        out_shape=tuple(jax.ShapeDtypeStruct(x.shape, x.dtype) for x in results),
+        in_specs=[vmem_spec] * 4,
+        out_specs=(any_spec,) * 4,
+        scratch_shapes=[dma((4,))],
+        compiler_params=pltpu.CompilerParams(vmem_limit_bytes=2**20),
+    )(*results)
+    return tuple(x[None, None] for x in outs)
+
+
+def body(activations, out_grads, next_inputs, counts, master, moment, second):
+    n = lax.axis_size("shard")
+    nz = n // columns_of(n)
+    whole_rows = activations.shape[3] == master.shape[2]
+    step = fused_body if whole_rows and nz & (nz - 1) == 0 else split_body
+    return step(activations, out_grads, next_inputs, counts, master, moment, second)
+
+
 def solution(mesh):
     spec = P("expert", "shard", None, None)
     return jax.shard_map(

time: 144 us -> 131 us (0.910)
  Pallas kernels: 138 us -> 129 us
  local copies, waits for them, and re-layouts: 3.94 us -> 0 us
    pallas_call x3 -> x2, Pallas kernels: 138 us -> 129 us  [the longest x1 123 us: fused_body(): pl.pallas_call(functools.partial(fused_kernel, n, ne, nx, entries, parts,...]
    unnamed x7 -> x0, local copies, waits for them, and re-layouts: 2.01 us -> none
    another operation x1 -> x0, local copies, waits for them, and re-layouts: 1.51 us -> none  [body(): projected[None, None]]
where the time goes in v1:
time: 131 us
  Pallas kernels  129 us (98%)
    pallas_call x1, Pallas kernels, fused_body(): pl.pallas_call(functools.partial(fused_kernel, n, ne, nx, entries, parts,...  123 us
    pallas_call x1, Pallas kernels, fused_body(): pl.pallas_call(store_kernel, out_shape=tuple((jax.ShapeDtypeStruct(x.shap...  5.74 us

profile of v1, /device:TPU:0, one launch (start us, length us, event | category | flops | bytes accessed | tf_op | source)
XLA Modules:
  0.0 130.5 jit_solution(11153584830422698466)
XLA Ops:
  1.3 123.5 %shard_map.102 = (f32[2048,896]{1,0:T(8,128)S(1)}, bf16[2048,896]{1,0:T(8,128)(2,1)S(1)}, bf16[2048,896]{1,0:T(8,128)(2,1)S(1)}, bf16[96,7168]{1,0:T(8,128)(2,1)S(1)}) custom-call(s32[1,1]{1,0:T(1,128)S(6)} %copy.11.cnt_hbm, bf16[96,2048]{1,0:T(8,128)(2,1)} %bitcast.14, bf16[96,7168]{1,0:T(8,128)(2,1)} %bitcast.13, bf16[96,2048]{1,0:T(8,128)(2,1)} %bitcast.15, ...), custom_call_target="tpu_custom_call" | custom-call | tf_op jit(solution)/shard_map/pallas_call | solution.py:714
  124.8 5.7 %shard_map.103 = (f32[2048,896]{1,0:T(8,128)}, bf16[2048,896]{1,0:T(8,128)(2,1)}, bf16[2048,896]{1,0:T(8,128)(2,1)}, bf16[96,7168]{1,0:T(8,128)(2,1)}) custom-call(f32[2048,896]{1,0:T(8,128)S(1)} %get-tuple-element.12.refs_0_, bf16[2048,896]{1,0:T(8,128)(2,1)S(1)} %get-tuple-element.13.refs_1_, bf16[2048,896]{1,0:T(8,128)(2,1)S(1)} %get-tuple-element.14.refs_2_, ...), custom_call_target="tpu_custom_call" | custom-call | tf_op jit(solution)/shard_map/pallas_call | solution.py:745

commit v2 on v1

--- a/solution.py
+++ b/solution.py
@@ -396,7 +396,7 @@
 
 
 def fused_kernel(
-    n, ne, nx, entries, parts, halves, pieces,
+    n, ne, nx, entries, parts, strips, pieces,
     cnt_hbm, act, cot_hbm, nxt, w_hbm, m_hbm, v_hbm,
     w_out, m_out, v_out, got,
     acts, nxt_all, cot_all, cots, w, wb, cnt, sq_src, sq_all, up_src, up_all,
@@ -464,48 +464,45 @@
     def z_slot(k):
         return lax.rem(iz + k + nz, nz) * nx + ix
 
-    def cut(buf, slot, p, count):
-        width = d_full // count
+    def cut(buf, slot, p):
+        width = d_full // parts
         return buf.at[slot, :, pl.ds(p * width, width)]
 
     def holds(h, t):
         return iz >= t if h == 0 else iz < nz - t
 
     def z_send(g, t, h, p):
-        buf, count, zs, zr, _, _ = g
+        buf, zs, zr, _, _ = g
         way = 1 - 2 * h
         slot = z_slot(-way * (t - 1))
         more = jnp.logical_and(iz >= t - 1, iz < nz - 1) if h == 0 else jnp.logical_and(iz <= nz - t, iz > 0)
-        block = cut(buf, slot, p, count)
+        block = cut(buf, slot, p)
         send(block, block, zs.at[h, t], zr.at[h, p, t], z_slot(way), when=more)
         if p == 0:
             drains.append((buf.at[slot], zs.at[h, t], more))
 
     def x_send(g, t, h, p):
-        buf, count, _, _, xs, xr = g
+        buf, _, _, xs, xr = g
         slot = z_slot(-(1 - 2 * h) * t)
         when = None if t == 0 else holds(h, t)
-        block = cut(buf, slot, p, count)
+        block = cut(buf, slot, p)
         for d in range(1, nx):
-            landing = xr.at[p] if buf is acts else xr.at[h, t, d - 1]
+            landing = xr.at[0] if buf is acts else xr.at[h, t, d - 1]
             send(block, block, xs.at[h, t, d - 1], landing, iz * nx + lax.rem(ix + d, nx), when=when)
             if p == 0:
                 drains.append((buf.at[slot], xs.at[h, t, d - 1], when))
 
-    def own_z(g, p):
-        if nz > 1:
-            for h in range(2):
-                z_send(g, 1, h, p)
-
     def own(g, ps):
         for p in ps:
-            own_z(g, p)
+            if nz > 1:
+                for h in range(2):
+                    z_send(g, 1, h, p)
             x_send(g, 0, 0, p)
 
     def relay(g, t, ps):
         for p in ps:
             for h in range(2):
-                await_copy(cut(g[0], z_slot(-(1 - 2 * h) * t), p, g[1]), g[3].at[h, p, t], holds(h, t))
+                await_copy(cut(g[0], z_slot(-(1 - 2 * h) * t), p), g[2].at[h, p, t], holds(h, t))
                 if t < nz - 1:
                     z_send(g, t + 1, h, p)
                 x_send(g, t, h, p)
@@ -513,15 +510,15 @@
     def peer_to(k, dx):
         return flip(iz, k, nz) * nx + lax.rem(ix + dx, nx)
 
-    def cot_sends(which):
-        for k, dx in which:
-            peer = peer_to(k, dx)
-            cols = pl.ds(pl.multiple_of(peer * f_blk, LANES), f_blk)
-            send(cots.at[:, cols], cot_all.at[me], cot_sem.at[0], cot_sem.at[1], peer)
-
-    g_acts = (acts, parts, az_send, az_recv, ax_send, ax_recv)
-    g_nxt = (nxt_all, halves, nz_send, nz_recv, nx_send, nx_recv)
-    every, each = range(parts), range(halves)
+    def cot_send(k, dx, q):
+        peer = peer_to(k, dx)
+        start, span = sum(strips[:q]), strips[q]
+        cols = pl.ds(pl.multiple_of(peer * f_blk + start, LANES), span)
+        send(cots.at[:, cols], cot_all.at[me, :, pl.ds(start, span)], cot_sem.at[0], cot_sem.at[1 + q], peer)
+
+    g_acts = (acts, az_send, az_recv, ax_send, ax_recv)
+    g_nxt = (nxt_all, nz_send, nz_recv, nx_send, nx_recv)
+    every = range(parts)
     tile = 64
 
     def w_body(i, acc):
@@ -529,43 +526,62 @@
         return acc + fold(x * x)
 
     zero = jnp.zeros((SUBLANES, LANES), jnp.float32)
-    far = sorted(range(1, nz), key=lambda k: (-k.bit_length(), k))
-    near = [(0, dx) for dx in range(1, nx)]
-    order = near + [(k, 0) for k in far] + [(k, dx) for k in far for dx in range(1, nx)]
-    share = -(-len(order) // max(nz - 1, 1))
-    cuts = [share * (t + 1) for t in range(nz)]
+    if nz == 4:
+        inner = lax.rem(lax.div(iz + 1, 2), 2)
+        ks = [1 + 2 * inner, 2, 3 - 2 * inner]
+    else:
+        ks = sorted(range(1, nz), key=lambda k: (-k.bit_length(), k))
+    others = range(1, nx)
+
+    def exchange(k, q):
+        for dx in range(nx):
+            cot_send(k, dx, q)
+
+    def near(q):
+        for dx in others:
+            cot_send(0, dx, q)
 
     own(g_acts, every)
-    cot_sends(order[: cuts[0]])
+    if nz > 1:
+        relay(g_acts, 1, every)
+        exchange(ks[0], 0)
     cot_all[me] = cots[:, pl.ds(pl.multiple_of(me * f_blk, LANES), f_blk)]
-    squares = zero
-    for t in range(1, nz):
+    loads[4].wait()
+    squares = lax.fori_loop(0, d_blk // tile, w_body, zero)
+    for t in range(2, nz - 1):
         relay(g_acts, t, every)
-        cot_sends(order[cuts[t - 1] : cuts[t]])
-        if t == 1:
-            loads[4].wait()
-            squares = lax.fori_loop(0, d_blk // tile, w_body, zero)
+    for k in ks[1:]:
+        exchange(k, 0)
+    near(0)
+    if nz > 2:
+        relay(g_acts, nz - 1, every)
+    for q in range(1, len(strips)):
+        for k in ks:
+            exchange(k, q)
+        near(q)
+    loads[3].wait()
+    own(g_nxt, every[:2])
     up_src[0:1] = jnp.sum(squares, axis=0, keepdims=True)
-    await_copy(cot_all.at[pl.ds(0, n - 1)], cot_sem.at[1])
-
-    g_tile = 256
+
+    g_tile = min(512, d_blk)
+
+    if nx > 1:
+        await_copy(acts.at[pl.ds(0, nz * (nx - 1))], ax_recv.at[0])
     total = zero
-    per = d_full // parts // g_tile
-
-    def g_body(i, acc):
-        rows = pl.ds(pl.multiple_of(i * g_tile, g_tile), g_tile)
-        g = lax.dot_general(
-            acts[:, :, rows].reshape(n * cap, g_tile), cot_all[...].reshape(n * cap, f_blk),
-            (((0,), (0,)), ((), ())), preferred_element_type=jnp.float32,
-        )
-        w_out[rows, :] = g
-        return acc + fold(g * g)
-
-    for p in every:
-        if nx > 1:
-            width = d_full // parts
-            await_copy(acts.at[pl.ds(0, nz * (nx - 1)), :, pl.ds(p * width, width)], ax_recv.at[p])
-        total = lax.fori_loop(p * per, (p + 1) * per, g_body, total)
+    for q, span in enumerate(strips):
+        cols = pl.ds(sum(strips[:q]), span)
+        await_copy(cot_all.at[pl.ds(0, n - 1), :, cols], cot_sem.at[1 + q])
+
+        def g_body(i, acc):
+            rows = pl.ds(pl.multiple_of(i * g_tile, g_tile), g_tile)
+            g = lax.dot_general(
+                acts[:, :, rows].reshape(n * cap, g_tile), cot_all[:, :, cols].reshape(n * cap, span),
+                (((0,), (0,)), ((), ())), preferred_element_type=jnp.float32,
+            )
+            w_out[rows, cols] = g
+            return acc + fold(g * g)
+
+        total = lax.fori_loop(0, d_blk // g_tile, g_body, total)
     sq_src[...] = jnp.sum(total, axis=0, keepdims=True)
     for de in range(ne):
         for ds in range(n):
@@ -574,8 +590,9 @@
                     sq_src, sq_all.at[de * n + ds], sq_sem.at[0], sq_sem.at[1],
                     lax.rem(me + ds, n), lax.rem(ex + de, ne),
                 )
-    loads[3].wait()
-    own(g_nxt, each)
+    own(g_nxt, every[2:])
+    if nz > 1:
+        relay(g_nxt, 1, every[:1])
     loads[5].wait()
     loads[6].wait()
     await_copy(sq_all.at[pl.ds(1, ne * n - 1)], sq_sem.at[1])
@@ -605,17 +622,18 @@
         return lax.fori_loop(first, last, u_body, acc)
 
     steps = d_blk // u_tile
-    early = 1
-    mid = steps * 3 // 4
+    mid = steps // 2
     acc = u_span(0, mid, zero)
     if nz > 1:
-        relay(g_nxt, 1, each[:early])
+        relay(g_nxt, 1, every[1:2])
     acc = u_span(mid, steps, acc)
     up_src[1:2] = jnp.sum(acc, axis=0, keepdims=True)
     for ds in range(1, n):
         send(up_src, up_all.at[ds], up_sem.at[0], up_sem.at[1], lax.rem(me + ds, n))
     if nz > 1:
-        relay(g_nxt, 1, each[early:])
+        relay(g_nxt, 1, every[2:])
+    if nz > 2:
+        relay(g_nxt, 2, every[:2])
     await_copy(up_all.at[pl.ds(1, n - 1)], up_sem.at[1])
     sums = up_src[...]
     for ds in range(1, n):
@@ -651,20 +669,14 @@
             start += piece
 
     if nz == 4:
-        inner = lax.rem(lax.div(iz + 1, 2), 2)
-        ks = [1 + 2 * inner, 2, 3 - 2 * inner]
-    else:
-        ks = far
-    others = range(1, nx)
-    if nz == 4:
         project(ks[0], 0)
-        relay(g_nxt, 2, each)
+        relay(g_nxt, 2, every[2:])
         project(ks[1], 0)
         crossed(0)
         crossed(1)
         for dx in others:
             project(ks[0], dx)
-        relay(g_nxt, 3, each)
+        relay(g_nxt, 3, every)
         project(ks[2], 0)
         crossed(2)
         for dx in others:
@@ -674,7 +686,7 @@
             project(ks[2], dx)
     else:
         for t in range(2, nz):
-            relay(g_nxt, t, each)
+            relay(g_nxt, t, every[2:] if t == 2 else every)
         for t in range(nz):
             crossed(t)
         for k in ks:
@@ -709,10 +721,10 @@
     dma = pltpu.SemaphoreType.DMA
     parts = 4
     pieces = split_lanes(f_blk, 2)
-    halves = 2
+    strips = split_lanes(f_blk, 3)[::-1]
     across = dma((2, nz, max(nx - 1, 1)))
     results = pl.pallas_call(
-        functools.partial(fused_kernel, n, ne, nx, entries, parts, halves, pieces),
+        functools.partial(fused_kernel, n, ne, nx, entries, parts, strips, pieces),
         out_shape=(
             pltpu.VMEM((d_blk, f_blk), f32),
             pltpu.VMEM((d_blk, f_blk), bf16),
@@ -735,9 +747,9 @@
             pltpu.VMEM((n, 2, LANES), f32),
             dma((7,)),
         ]
-        + [dma((2, nz)), dma((2, parts, nz)), across, dma((parts,))]
-        + [dma((2, nz)), dma((2, halves, nz)), across, across]
-        + [dma((2,))] * 4,
+        + [dma((2, nz)), dma((2, parts, nz)), across, dma((1,))]
+        + [dma((2, nz)), dma((2, parts, nz)), across, across]
+        + [dma((1 + len(strips),))] + [dma((2,))] * 3,
         compiler_params=pltpu.CompilerParams(
             collective_id=0, has_side_effects=True, vmem_limit_bytes=47 * 2**20
         ),

time: 131 us -> 119 us (0.908)
  Pallas kernels: 129 us -> 118 us
    pallas_call x1, Pallas kernels: 123 us -> 112 us  [fused_body(): pl.pallas_call(functools.partial(fused_kernel, n, ne, nx, entries, parts,...]
where the time goes in v2:
time: 119 us
  Pallas kernels  118 us (99%)
  between operations  1.29 us (1%)
    pallas_call x1, Pallas kernels, fused_body(): pl.pallas_call(functools.partial(fused_kernel, n, ne, nx, entries, parts,...  112 us
    pallas_call x1, Pallas kernels, fused_body(): pl.pallas_call(store_kernel, out_shape=tuple((jax.ShapeDtypeStruct(x.shap...  5.74 us

profile of v2, /device:TPU:0, one launch (start us, length us, event | category | flops | bytes accessed | tf_op | source)
XLA Modules:
  0.0 119.3 jit_solution(311923595845300642)
XLA Ops:
  1.3 112.3 %shard_map.102 = (f32[2048,896]{1,0:T(8,128)S(1)}, bf16[2048,896]{1,0:T(8,128)(2,1)S(1)}, bf16[2048,896]{1,0:T(8,128)(2,1)S(1)}, bf16[96,7168]{1,0:T(8,128)(2,1)S(1)}) custom-call(s32[1,1]{1,0:T(1,128)S(6)} %copy.11.cnt_hbm, bf16[96,2048]{1,0:T(8,128)(2,1)} %bitcast.14, bf16[96,7168]{1,0:T(8,128)(2,1)} %bitcast.13, bf16[96,2048]{1,0:T(8,128)(2,1)} %bitcast.15, ...), custom_call_target="tpu_custom_call" | custom-call | tf_op jit(solution)/shard_map/pallas_call | solution.py:726
  113.5 5.7 %shard_map.103 = (f32[2048,896]{1,0:T(8,128)}, bf16[2048,896]{1,0:T(8,128)(2,1)}, bf16[2048,896]{1,0:T(8,128)(2,1)}, bf16[96,7168]{1,0:T(8,128)(2,1)}) custom-call(f32[2048,896]{1,0:T(8,128)S(1)} %get-tuple-element.12.refs_0_, bf16[2048,896]{1,0:T(8,128)(2,1)S(1)} %get-tuple-element.13.refs_1_, bf16[2048,896]{1,0:T(8,128)(2,1)S(1)} %get-tuple-element.14.refs_2_, ...), custom_call_target="tpu_custom_call" | custom-call | tf_op jit(solution)/shard_map/pallas_call | solution.py:757

commit v3 on v2

--- a/solution.py
+++ b/solution.py
@@ -563,7 +563,7 @@
     own(g_nxt, every[:2])
     up_src[0:1] = jnp.sum(squares, axis=0, keepdims=True)
 
-    g_tile = min(512, d_blk)
+    g_tile = min(1024, d_blk)
 
     if nx > 1:
         await_copy(acts.at[pl.ds(0, nz * (nx - 1))], ax_recv.at[0])
@@ -602,7 +602,7 @@
     rms = jnp.sqrt(jnp.sum(norm, keepdims=True) / entries + 1e-06)
     clip = jnp.minimum(1.0, 1.0 / rms)
 
-    u_tile = 32
+    u_tile = 64
     first_scale, later_scale = 1.0 / (1.0 - 0.9**10), 1.0 / (1.0 - 0.999**10)
 
     def u_body(i, acc):

time: 119 us -> 118 us (level)
  no operation moved by 1% of the time
where the time goes in v3:
time: 118 us
  Pallas kernels  117 us (99%)
  between operations  1.29 us (1%)
    pallas_call x1, Pallas kernels, fused_body(): pl.pallas_call(functools.partial(fused_kernel, n, ne, nx, entries, parts,...  111 us
    pallas_call x1, Pallas kernels, fused_body(): pl.pallas_call(store_kernel, out_shape=tuple((jax.ShapeDtypeStruct(x.shap...  5.74 us

profile of v3, /device:TPU:0, one launch (start us, length us, event | category | flops | bytes accessed | tf_op | source)
XLA Modules:
  0.0 118.3 jit_solution(6334573267591189408)
XLA Ops:
  1.3 111.3 %shard_map.102 = (f32[2048,896]{1,0:T(8,128)S(1)}, bf16[2048,896]{1,0:T(8,128)(2,1)S(1)}, bf16[2048,896]{1,0:T(8,128)(2,1)S(1)}, bf16[96,7168]{1,0:T(8,128)(2,1)S(1)}) custom-call(s32[1,1]{1,0:T(1,128)S(6)} %copy.11.cnt_hbm, bf16[96,2048]{1,0:T(8,128)(2,1)} %bitcast.14, bf16[96,7168]{1,0:T(8,128)(2,1)} %bitcast.13, bf16[96,2048]{1,0:T(8,128)(2,1)} %bitcast.15, ...), custom_call_target="tpu_custom_call" | custom-call | tf_op jit(solution)/shard_map/pallas_call | solution.py:726
  112.6 5.7 %shard_map.103 = (f32[2048,896]{1,0:T(8,128)}, bf16[2048,896]{1,0:T(8,128)(2,1)}, bf16[2048,896]{1,0:T(8,128)(2,1)}, bf16[96,7168]{1,0:T(8,128)(2,1)}) custom-call(f32[2048,896]{1,0:T(8,128)S(1)} %get-tuple-element.12.refs_0_, bf16[2048,896]{1,0:T(8,128)(2,1)S(1)} %get-tuple-element.13.refs_1_, bf16[2048,896]{1,0:T(8,128)(2,1)S(1)} %get-tuple-element.14.refs_2_, ...), custom_call_target="tpu_custom_call" | custom-call | tf_op jit(solution)/shard_map/pallas_call | solution.py:757
